TPU v7x, 512 devices: a whole 4x8x8 slice. The times are simulated.
512 devices in a mesh: expert: 8 (over x, core), dp: 64 (over z, y).
Axes of the slice: x: 4, y: 8, z: 8, core: 2. Of those that a mesh axis runs over, the one named last changes fastest.
Arguments:
- tokens: bfloat16 [4096, 4096], P(('expert', 'dp')), may hold values from -6 to 6
- expert_ids: int32 [4096, 2], P(('expert', 'dp')), may hold values from 0 to 7, as said below
- slots: int32 [4096, 2], P(('expert', 'dp')), may hold values from -1 to 1, as said below
- mix_weights: float32 [4096, 2], P(('expert', 'dp')), may hold values from 0.1 to 1
- w_gate: bfloat16 [8, 4096, 8192], P('expert', None, 'dp'), may hold values from -0.09375 to 0.09375
- w_up: bfloat16 [8, 4096, 8192], P('expert', None, 'dp'), may hold values from -0.09375 to 0.09375
- w_down: bfloat16 [8, 8192, 4096], P('expert', None, 'dp'), may hold values from -0.0625 to 0.0625
Outputs:
- mixed: bfloat16 [4096, 4096], P(('expert', 'dp'))
Inputs may be any that keep to these rules, and one draw needn't show every extreme that they name: `expert_ids`: each token names 2 different experts. Within each aligned block of 8 tokens (the tokens of one device), the assignments to one expert get distinct slots among 0 to 1 in some order, at most 2 of them are kept and the others get -1; an expert with 2 or more assignments in the block has all 2 slots used. No two assignments of one block share an expert and a slot. In every block some expert has all 2 slots used.
All inputs are finite; a program needn't handle non-finite values.
Results may differ from a plain program's by a relative error of at most 0.0085.
Values may be sent and summed in bfloat16 or wider, within the bound.
No kernel may reach another device: no remote copies, remote signals or barrier semaphores. Data moves between devices by JAX's collectives and lax.ppermute only.
A program may use at most 128 MiB of HBM per device.

v0:
```python
import jax
import jax.numpy as jnp
from jax import lax
from jax.sharding import PartitionSpec as P

CAP = 2


def shards(tokens, expert_ids, slots, mix_weights, w_gate, w_up, w_down):
    tok_rows, model_width = tokens.shape
    experts = lax.axis_size("expert")
    capacity = CAP
    slot_count = experts * capacity
    slot_ids = jnp.arange(slot_count, dtype=jnp.int32)
    slot_expert = slot_ids // capacity
    slot_index = slot_ids % capacity
    matches = (expert_ids[None, :, :] == slot_expert[:, None, None]) & (
        slots[None, :, :] == slot_index[:, None, None]
    )
    occupied = jnp.any(matches, axis=2)
    dispatch_table = occupied.astype(jnp.bfloat16)
    outgoing = jnp.dot(dispatch_table, tokens, preferred_element_type=jnp.float32).astype(
        jnp.bfloat16
    )
    arrived = lax.all_to_all(outgoing, "expert", split_axis=0, concat_axis=0, tiled=True)
    gate_w = w_gate[0]
    up_w = w_up[0]
    down_w = w_down[0]
    portion = lax.all_gather(arrived, "dp", axis=0, tiled=True)
    gate_part = jnp.dot(portion, gate_w, preferred_element_type=jnp.float32)
    up_part = jnp.dot(portion, up_w, preferred_element_type=jnp.float32)
    hidden = (jax.nn.silu(gate_part) * up_part).astype(jnp.bfloat16)
    summed = jnp.dot(
        lax.all_gather(hidden, "dp", axis=1, tiled=True), down_w, preferred_element_type=jnp.float32
    )
    result = summed.astype(jnp.bfloat16)
    groups = lax.axis_size("dp")
    blocks = result.reshape(groups, experts, capacity, result.shape[1])
    blocks = lax.all_to_all(blocks, "expert", split_axis=1, concat_axis=1, tiled=True)
    blocks = lax.all_to_all(blocks, "dp", split_axis=0, concat_axis=3, tiled=True)
    returned = blocks.reshape(slot_count, model_width)
    weight_table = jnp.sum(jnp.where(matches, mix_weights[None, :, :], 0.0), axis=2)
    mixed = jnp.dot(
        weight_table.T, returned.astype(jnp.float32), preferred_element_type=jnp.float32
    )
    return mixed.astype(jnp.bfloat16)


def solution(mesh):
    placed = (
        P(("expert", "dp"), None),
        P(("expert", "dp"), None),
        P(("expert", "dp"), None),
        P(("expert", "dp"), None),
        P("expert", None, "dp"),
        P("expert", None, "dp"),
        P("expert", None, "dp"),
    )
    return jax.shard_map(
        shards, mesh=mesh, in_specs=placed, out_specs=P(("expert", "dp"), None), check_vma=False
    )
```

profile of v0, /device:TPU:1, one launch (start us, length us, event | category | flops | bytes accessed | tf_op | source)
XLA Modules:
  0.0 327.1 jit_solution(15211576409830812576)
XLA Ops:
  6.5 0.0 copy-start
  6.5 0.0 copy-start.6
  6.5 0.0 all-gather.3.cloned.1.call-start
  6.5 0.9 fusion.5
  7.5 1.1 convolution_convert_fusion
  8.5 0.1 all_to_all.22
  8.6 14.5 %all_to_all.32 = bf16[8,2,4096]{2,1,0:T(2,128)(2,1)S(1)} all-to-all(bf16[8,2,4096]{2,1,0:T(2,128)(2,1)S(1)} %all_to_all.22), channel_id=1, replica_groups=mesh['expert'=8,'dp'=64] {'expert'}, dimensions={0} | all-to-all | bytes 262144 | tf_op jit(solution)/shard_map/all_to_all | solution.py:25
  23.1 0.7 all_to_all.24
  23.8 0.0 all-gather.3.cloned.1.call-update
  23.8 0.0 all-gather.5.cloned.1.call-start
  23.9 98.3 %all-gather.3.cloned.1.call-done = bf16[1024,4096]{1,0:T(8,128)(2,1)} async-done(((bf16[16,4096]{1,0:T(8,128)(2,1)}), bf16[1024,4096]{1,0:T(8,128)(2,1)}) %all-gather.3.cloned.1.call-update) | async-done | bytes 8388624 | tf_op jit(solution)/shard_map/all_gather | solution.py:29
  122.2 0.0 copy-done
  122.2 0.0 copy-start.5
  122.2 5.8 %fusion.3 = f32[1024,128]{1,0:T(8,128)S(1)} fusion(bf16[1024,4096]{1,0:T(8,128)(2,1)} %all-gather.3.cloned.1.call-done, bf16[1,4096,128]{2,1,0:T(8,128)(2,1)S(1)} %copy-done), kind=kOutput, calls=%fused_computation.7 | convolution fusion | flops 1073741824 | bytes 9961472 | tf_op jit(solution)/shard_map/dot_general | solution.py:30
  128.1 0.0 copy-done.6
  128.1 0.0 copy-done.5
  128.1 0.0 copy-start.1
  128.1 3.0 fusion
  131.1 0.0 all-gather.5.cloned.1.call-update
  131.2 0.0 copy-start.2
  131.2 0.0 copy-start.3
  131.2 0.0 copy-start.4
  131.2 141.9 %all-gather.5.cloned.1.call-done = bf16[1024,8192]{1,0:T(8,128)(2,1)} async-done(((bf16[1024,128]{1,0:T(8,128)(2,1)}), bf16[1024,8192]{1,0:T(8,128)(2,1)}) %all-gather.5.cloned.1.call-update) | async-done | bytes 16777232 | tf_op jit(solution)/shard_map/all_gather | solution.py:34
  273.1 0.0 copy-done.1
  273.1 10.9 %convolution_convert_fusion.2 = bf16[1024,64]{0,1:T(8,128)(2,1)S(1)} fusion(bf16[1024,8192]{1,0:T(8,128)(2,1)} %all-gather.5.cloned.1.call-done, bf16[1,8192,64]{1,2,0:T(8,128)(2,1)S(1)} %copy-done.1), kind=kOutput, calls=%fused_computation.4 | convolution fusion | flops 1073807360 | bytes 17956864 | tf_op jit(solution)/shard_map/dot_general | solution.py:33
  284.1 0.2 copy.29
  284.3 0.2 copy.34
  284.4 0.2 reshape.36
  284.7 13.9 %all_to_all.33 = bf16[8,2,4096]{2,1,0:T(2,128)(2,1)S(1)} all-to-all(bf16[8,2,4096]{2,1,0:T(2,128)(2,1)S(1)} %reshape.36), channel_id=1, replica_groups=mesh['expert'=8,'dp'=64] {'expert'}, dimensions={0} | all-to-all | bytes 262144 | tf_op jit(solution)/shard_map/all_to_all | solution.py:39
  298.6 0.2 reshape.37
  298.9 0.2 copy.31
  299.0 0.8 reshape.38
  299.9 7.4 %all-to-all-start.2 = ((bf16[64,2,512]{2,1,0:T(2,128)(2,1)}), bf16[64,2,512]{2,1,0:T(2,128)(2,1)S(1)}, u32[]{:S(2)}, u32[]{:S(2)}) async-start(bf16[64,2,512]{2,1,0:T(2,128)(2,1)} %reshape.38), calls=%async_computation.2 | async-start | bytes 262144 | tf_op jit(solution)/shard_map/all_to_all | solution.py:40
  307.2 0.0 copy-done.2
  307.3 0.0 copy-done.3
  307.3 0.0 copy-done.4
  307.3 0.1 select_reduce_fusion
  307.4 11.5 %all-to-all-done.2 = bf16[64,2,512]{2,1,0:T(2,128)(2,1)S(1)} async-done(((bf16[64,2,512]{2,1,0:T(2,128)(2,1)}), bf16[64,2,512]{2,1,0:T(2,128)(2,1)S(1)}, u32[]{:S(2)}, u32[]{:S(2)}) %all-to-all-start.2) | async-done | bytes 131104 | tf_op jit(solution)/shard_map/all_to_all | solution.py:40
  318.9 0.2 reshape.39
  319.1 0.1 copy.32
  319.2 0.3 reshape.35
  319.4 0.8 fusion.6
  (1 shorter events, 0.0 us)
Async XLA Ops:
  6.5 115.7 %copy-start = (bf16[1,4096,128]{2,1,0:T(8,128)(2,1)S(1)}, bf16[1,4096,128]{2,1,0:T(8,128)(2,1)}, u32[]{:S(2)}) copy-start(bf16[1,4096,128]{2,1,0:T(8,128)(2,1)} %param.11) | copy-start | bytes 3145732
  6.5 121.5 %copy-start.6 = (bf16[1,4096,128]{2,1,0:T(8,128)(2,1)S(1)}, bf16[1,4096,128]{2,1,0:T(8,128)(2,1)}, u32[]{:S(2)}) copy-start(bf16[1,4096,128]{2,1,0:T(8,128)(2,1)} %param.12) | copy-start | bytes 3145732
  6.5 115.7 %all-gather.3.cloned.1.call-start = ((), (), s32[]{:S(2)}) async-start(), calls=%async_computation.3 | async-start | bytes 8519680 | tf_op jit(solution)/shard_map/all_gather | solution.py:29
  23.8 249.3 %all-gather.5.cloned.1.call-start = ((), (), s32[]{:S(2)}) async-start(), calls=%async_computation.4 | async-start | bytes 17039360 | tf_op jit(solution)/shard_map/all_gather | solution.py:34
  122.2 5.9 %copy-start.5 = (bf16[1024,4096]{1,0:T(8,128)(2,1)S(1)}, bf16[1024,4096]{1,0:T(8,128)(2,1)}, u32[]{:S(2)}) copy-start(bf16[1024,4096]{1,0:T(8,128)(2,1)} %all-gather.3.cloned.1.call-done) | copy-start | bytes 25165828
  128.1 145.1 %copy-start.1 = (bf16[1,8192,64]{1,2,0:T(8,128)(2,1)S(1)}, bf16[1,8192,64]{1,2,0:T(8,128)(2,1)}, u32[]{:S(2)}) copy-start(bf16[1,8192,64]{1,2,0:T(8,128)(2,1)} %param.13) | copy-start | bytes 3145732
  131.2 176.1 %copy-start.2 = (s32[8,2]{0,1:T(2,128)S(1)}, s32[8,2]{0,1:T(2,128)}, u32[]{:S(2)}) copy-start(s32[8,2]{0,1:T(2,128)} %param.9) | copy-start | bytes 196
  131.2 176.1 %copy-start.3 = (s32[8,2]{0,1:T(2,128)S(1)}, s32[8,2]{0,1:T(2,128)}, u32[]{:S(2)}) copy-start(s32[8,2]{0,1:T(2,128)} %param.8) | copy-start | bytes 196
  131.2 176.1 %copy-start.4 = (f32[8,2]{0,1:T(2,128)S(1)}, f32[8,2]{0,1:T(2,128)}, u32[]{:S(2)}) copy-start(f32[8,2]{0,1:T(2,128)} %param.10) | copy-start | bytes 196
  299.9 19.0 %all-to-all-start.2 = ((bf16[64,2,512]{2,1,0:T(2,128)(2,1)}), bf16[64,2,512]{2,1,0:T(2,128)(2,1)S(1)}, u32[]{:S(2)}, u32[]{:S(2)}) async-start(bf16[64,2,512]{2,1,0:T(2,128)(2,1)} %reshape.38), calls=%async_computation.2 | async-start | bytes 262144 | tf_op jit(solution)/shard_map/all_to_all | solution.py:40
Sparse Core Ops, SparseCore 0:
  24.0 98.1 all-gather.2
  131.3 141.7 all-gather.4
where the time goes:
time: 327 us
  waiting for transfers between devices  252 us (77%)
  blocking collectives  28.4 us (9%)
  matrix products  21.7 us (7%)
  between operations  13.6 us (4%)
  starting transfers between devices  7.4 us (2%)
    all_gather x1, waiting for transfers between devices, shards(): lax.all_gather(hidden, 'dp', axis=1, tiled=True)  142 us
    all_gather x1, waiting for transfers between devices, shards(): portion = lax.all_gather(arrived, 'dp', axis=0, tiled=True)  98.3 us
    all_to_all x1, blocking collectives, shards(): lax.all_to_all(outgoing, 'expert', split_axis=0, concat_axis=0, tiled=True)  14.5 us
    all_to_all x1, blocking collectives, shards(): lax.all_to_all(blocks, 'expert', split_axis=1, concat_axis=1, tiled=True)  13.9 us
    all_to_all x1, waiting for transfers between devices, shards(): lax.all_to_all(blocks, 'dp', split_axis=0, concat_axis=3, tiled=True)  11.5 us
    dot_general x1, matrix products, shards(): jnp.dot(lax.all_gather(hidden, 'dp', axis=1, tiled=True), down_w, preferr...  10.9 us
    all_to_all x1, starting transfers between devices, shards(): lax.all_to_all(blocks, 'dp', split_axis=0, concat_axis=3, tiled=True)  7.36 us
  transfers between devices with their start and end apart: 3, of which 3 were waited for; matrix products, arithmetic and copies ran while one was open for 0% of the time, Pallas kernels for 0%

commit v1 on v0

--- a/solution.py
+++ b/solution.py
@@ -31,7 +31,11 @@
     up_part = jnp.dot(portion, up_w, preferred_element_type=jnp.float32)
     hidden = (jax.nn.silu(gate_part) * up_part).astype(jnp.bfloat16)
     summed = jnp.dot(
-        lax.all_gather(hidden, "dp", axis=1, tiled=True), down_w, preferred_element_type=jnp.float32
+        jnp.concatenate(
+            lax.all_to_all(jnp.stack([hidden] * lax.axis_size("dp")), "dp", 0, 0), axis=1
+        ),
+        down_w,
+        preferred_element_type=jnp.float32,
     )
     result = summed.astype(jnp.bfloat16)
     groups = lax.axis_size("dp")

time: 327 us -> 589 us (1.80)
  blocking collectives: 28.4 us -> 405 us
  waiting for transfers between devices: 252 us -> 110 us
  starting transfers between devices: 7.4 us -> 37.7 us
  matrix products: 21.7 us -> 13.1 us
  local copies, waits for them, and re-layouts: 3.24 us -> 9.32 us
    all_to_all x0 -> x1, blocking collectives: none -> 378 us  [shards(): lax.all_to_all(jnp.stack([hidden] * lax.axis_size('dp')), 'dp', 0, 0)]
    all_gather x1 -> x0, waiting for transfers between devices: 142 us -> none  [shards(): lax.all_gather(hidden, 'dp', axis=1, tiled=True)]
    all_to_all x1, starting transfers between devices: 7.36 us -> 37.7 us  [shards(): lax.all_to_all(blocks, 'dp', split_axis=0, concat_axis=3, tiled=True)]
    dot_general x1, matrix products: 10.9 us -> 3.02 us  [shards(): jnp.dot(jnp.concatenate(lax.all_to_all(jnp.stack([hidden] * lax.axis_size...]
    another operation x0 -> x1, local copies, waits for them, and re-layouts: none -> 5.96 us  [shards(): jnp.stack([hidden] * lax.axis_size('dp'))]
  transfers between devices with their start and end apart: 3 -> 2, of which waited for: 3 -> 2; matrix products, arithmetic and copies ran while one was open for 0% -> 0% of each run, Pallas kernels for 0% -> 0%
where the time goes in v1:
time: 589 us
  blocking collectives  405 us (69%)
  waiting for transfers between devices  110 us (19%)
  starting transfers between devices  37.7 us (6%)
  between operations  13.5 us (2%)
  matrix products  13.1 us (2%)
  local copies, waits for them, and re-layouts  9.32 us (2%)
    all_to_all x1, blocking collectives, shards(): lax.all_to_all(jnp.stack([hidden] * lax.axis_size('dp')), 'dp', 0, 0)  378 us
    all_gather x1, waiting for transfers between devices, shards(): portion = lax.all_gather(arrived, 'dp', axis=0, tiled=True)  98.3 us
    all_to_all x1, starting transfers between devices, shards(): lax.all_to_all(blocks, 'dp', split_axis=0, concat_axis=3, tiled=True)  37.7 us
    all_to_all x1, blocking collectives, shards(): lax.all_to_all(outgoing, 'expert', split_axis=0, concat_axis=0, tiled=True)  14.5 us
    all_to_all x1, blocking collectives, shards(): lax.all_to_all(blocks, 'expert', split_axis=1, concat_axis=1, tiled=True)  11.8 us
  transfers between devices with their start and end apart: 2, of which 2 were waited for; matrix products, arithmetic and copies ran while one was open for 0% of the time, Pallas kernels for 0%

profile of v1, /device:TPU:1, one launch (start us, length us, event | category | flops | bytes accessed | tf_op | source)
XLA Modules:
  0.0 589.1 jit_solution(18329901595103180858)
XLA Ops:
  6.5 0.0 copy-start
  6.5 0.0 copy-start.6
  6.5 0.0 all-gather.2.cloned.1.call-start
  6.5 0.9 fusion.5
  7.5 1.1 convolution_convert_fusion
  8.5 0.1 all_to_all.25
  8.6 14.5 %all_to_all.37 = bf16[8,2,4096]{2,1,0:T(2,128)(2,1)S(1)} all-to-all(bf16[8,2,4096]{2,1,0:T(2,128)(2,1)S(1)} %all_to_all.25), channel_id=1, replica_groups=mesh['expert'=8,'dp'=64] {'expert'}, dimensions={0} | all-to-all | bytes 262144 | tf_op jit(solution)/shard_map/all_to_all | solution.py:25
  23.1 0.7 all_to_all.27
  23.8 0.0 all-gather.2.cloned.1.call-update
  23.8 98.3 %all-gather.2.cloned.1.call-done = bf16[1024,4096]{1,0:T(8,128)(2,1)} async-done(((bf16[16,4096]{1,0:T(8,128)(2,1)}), bf16[1024,4096]{1,0:T(8,128)(2,1)}) %all-gather.2.cloned.1.call-update) | async-done | bytes 8388624 | tf_op jit(solution)/shard_map/all_gather | solution.py:29
  122.2 0.0 copy-done
  122.2 0.0 copy-start.5
  122.2 5.9 fusion.3
  128.0 0.0 copy-done.6
  128.1 0.0 copy-done.5
  128.1 2.3 fusion
  130.4 0.1 copy.32
  130.6 6.0 %stack.2 = bf16[64,1024,128]{1,2,0:T(8,128)(2,1)} broadcast(bf16[1024,128]{0,1:T(8,128)(2,1)S(1)} %copy.32), dimensions={1,2} | broadcast | bytes 17039360 | tf_op jit(solution)/shard_map/stack | solution.py:35
  136.5 0.0 copy-start.1
  136.5 378.3 %all_to_all.38 = bf16[64,1024,128]{1,2,0:T(8,128)(2,1)S(1)} all-to-all(bf16[64,1024,128]{1,2,0:T(8,128)(2,1)} %stack.2), channel_id=1, replica_groups=mesh['expert'=8,'dp'=64] {'dp'}, dimensions={0} | all-to-all | bytes 33554432 | tf_op jit(solution)/shard_map/all_to_all | solution.py:35
  514.8 0.0 copy-done.1
  514.8 0.0 copy-start.2
  514.8 0.0 copy-start.3
  514.8 0.0 copy-start.4
  514.8 3.0 convolution_convert_fusion.2
  517.9 0.2 copy.33
  518.0 0.2 copy.38
  518.2 0.2 reshape.46
  518.5 11.8 %all_to_all.39 = bf16[8,2,4096]{2,1,0:T(2,128)(2,1)S(1)} all-to-all(bf16[8,2,4096]{2,1,0:T(2,128)(2,1)S(1)} %reshape.46), channel_id=1, replica_groups=mesh['expert'=8,'dp'=64] {'expert'}, dimensions={0} | all-to-all | bytes 262144 | tf_op jit(solution)/shard_map/all_to_all | solution.py:43
  530.3 0.2 reshape.47
  530.5 0.2 copy.35
  530.7 0.8 reshape.48
  531.6 37.7 %all-to-all-start.3 = ((bf16[64,2,512]{2,1,0:T(2,128)(2,1)}), bf16[64,2,512]{2,1,0:T(2,128)(2,1)S(1)}, u32[]{:S(2)}, u32[]{:S(2)}) async-start(bf16[64,2,512]{2,1,0:T(2,128)(2,1)} %reshape.48), calls=%async_computation.3 | async-start | bytes 262144 | tf_op jit(solution)/shard_map/all_to_all | solution.py:44
  569.2 0.0 copy-done.2
  569.3 0.0 copy-done.3
  569.3 0.0 copy-done.4
  569.3 0.1 select_reduce_fusion
  569.4 11.5 %all-to-all-done.3 = bf16[64,2,512]{2,1,0:T(2,128)(2,1)S(1)} async-done(((bf16[64,2,512]{2,1,0:T(2,128)(2,1)}), bf16[64,2,512]{2,1,0:T(2,128)(2,1)S(1)}, u32[]{:S(2)}, u32[]{:S(2)}) %all-to-all-start.3) | async-done | bytes 131104 | tf_op jit(solution)/shard_map/all_to_all | solution.py:44
  580.9 0.2 reshape.49
  581.1 0.1 copy.36
  581.2 0.3 reshape.45
  581.4 0.8 fusion.6
  (1 shorter events, 0.0 us)
Async XLA Ops:
  6.5 115.6 %copy-start = (bf16[1,4096,128]{2,1,0:T(8,128)(2,1)S(1)}, bf16[1,4096,128]{2,1,0:T(8,128)(2,1)}, u32[]{:S(2)}) copy-start(bf16[1,4096,128]{2,1,0:T(8,128)(2,1)} %param.11) | copy-start | bytes 3145732
  6.5 121.5 %copy-start.6 = (bf16[1,4096,128]{2,1,0:T(8,128)(2,1)S(1)}, bf16[1,4096,128]{2,1,0:T(8,128)(2,1)}, u32[]{:S(2)}) copy-start(bf16[1,4096,128]{2,1,0:T(8,128)(2,1)} %param.12) | copy-start | bytes 3145732
  6.5 115.6 %all-gather.2.cloned.1.call-start = ((), (), s32[]{:S(2)}) async-start(), calls=%async_computation.4 | async-start | bytes 8519680 | tf_op jit(solution)/shard_map/all_gather | solution.py:29
  122.2 5.9 copy-start.5
  136.5 378.3 %copy-start.1 = (bf16[1,8192,64]{1,2,0:T(8,128)(2,1)S(1)}, bf16[1,8192,64]{1,2,0:T(8,128)(2,1)}, u32[]{:S(2)}) copy-start(bf16[1,8192,64]{1,2,0:T(8,128)(2,1)} %param.13) | copy-start | bytes 3145732
  514.8 54.4 %copy-start.2 = (s32[8,2]{0,1:T(2,128)S(1)}, s32[8,2]{0,1:T(2,128)}, u32[]{:S(2)}) copy-start(s32[8,2]{0,1:T(2,128)} %param.9) | copy-start | bytes 196
  514.8 54.4 %copy-start.3 = (s32[8,2]{0,1:T(2,128)S(1)}, s32[8,2]{0,1:T(2,128)}, u32[]{:S(2)}) copy-start(s32[8,2]{0,1:T(2,128)} %param.8) | copy-start | bytes 196
  514.8 54.4 %copy-start.4 = (f32[8,2]{0,1:T(2,128)S(1)}, f32[8,2]{0,1:T(2,128)}, u32[]{:S(2)}) copy-start(f32[8,2]{0,1:T(2,128)} %param.10) | copy-start | bytes 196
  531.6 49.3 %all-to-all-start.3 = ((bf16[64,2,512]{2,1,0:T(2,128)(2,1)}), bf16[64,2,512]{2,1,0:T(2,128)(2,1)S(1)}, u32[]{:S(2)}, u32[]{:S(2)}) async-start(bf16[64,2,512]{2,1,0:T(2,128)(2,1)} %reshape.48), calls=%async_computation.3 | async-start | bytes 262144 | tf_op jit(solution)/shard_map/all_to_all | solution.py:44
Sparse Core Ops, SparseCore 0:
  23.9 98.1 all-gather.1
